TPU v7x, 32 devices: a whole 2x2x4 slice. The times are simulated.
32 devices in a mesh: row: 4 (over z), col: 8 (over y, x, core).
Axes of the slice: x: 2, y: 2, z: 4, core: 2. Of those that a mesh axis runs over, the one named last changes fastest.
Arguments:
- matrix: float32 [8192, 8192], P('row', 'col'), may hold values from -2.5 to 2.5
Outputs:
- squared: float32 [8192, 8192], P('row', 'col')
- frob: float32 [], replicated
All inputs are finite; a program needn't handle non-finite values.
Results may differ from a plain program's by a relative error of at most 0.0001.
Values sent between devices are 32-bit elements; how exact they have to be, the bound alone decides.
A program may use at most 64 MiB of HBM per device.

v0:
```python
import jax
import jax.numpy as jnp
from jax import lax
from jax.sharding import PartitionSpec as P

KP = 256


def broadcast(value, axis, source):
    kept = jnp.where(lax.axis_index(axis) == source, value, 0).astype(value.dtype)
    return lax.psum(kept, axis)


def offsets(matrix, step):
    row_block = matrix.shape[0]
    col_block = matrix.shape[1]
    total = row_block * lax.axis_size("row")
    start = step * (total // 4)
    return (start // col_block, start % col_block, start // row_block, start % row_block)


def fetch_rows(matrix, step):
    col_owner, local_col, row_owner, local_row = offsets(matrix, step)
    return broadcast(matrix[local_row : local_row + KP, :], "row", row_owner)


def product(left, right):
    return jnp.dot(left, right, preferred_element_type=jnp.float32, precision=lax.Precision.HIGHEST)


def body(matrix):
    column_index = lax.axis_index("col")
    slots = []
    for step in range(4):
        col_owner, local_col, row_owner, local_row = offsets(matrix, step)
        panel = matrix[:, local_col : local_col + KP]
        slots.append(jnp.where(column_index == col_owner, panel, jnp.zeros_like(panel)))
    stacked = lax.psum(jnp.concatenate(slots, axis=1), "col")
    rights = jnp.concatenate([fetch_rows(matrix, step) for step in range(4)], axis=0)
    squared = product(stacked, rights)
    total = lax.psum(jnp.sum(squared * squared), ("row", "col"))
    order_size = matrix.shape[0] * lax.axis_size("row")
    frob = jnp.sqrt(total) / order_size
    return (squared, frob)


def solution(mesh):
    placed = (P("row", "col"),)
    return jax.shard_map(
        body, mesh=mesh, in_specs=placed, out_specs=(P("row", "col"), P()), check_vma=False
    )
```

profile of v0, /device:TPU:0, one launch (start us, length us, event | category | flops | bytes accessed | tf_op | source)
XLA Modules:
  0.0 378.5 jit_solution(3300064162137872236)
XLA Ops:
  7.2 0.0 all-reduce.6.cloned.1.call-start
  7.2 3.4 slice_select_fusion.7
  10.7 0.0 all-reduce.6.cloned.1.call-update
  10.7 0.0 all-reduce.4.cloned.1.call-start
  10.7 2.2 slice_select_fusion.3
  13.0 4.1 %pad_maximum_fusion = f32[2048,1024]{1,0:T(8,128)} fusion(f32[2048,256]{1,0:T(8,128)S(1)} %get-tuple-element.13, f32[2048,256]{1,0:T(8,128)S(1)} %get-tuple-element.12, f32[2048,256]{1,0:T(8,128)S(1)} %get-tuple-element.11, f32[2048,256]{1,0:T(8,128)S(1)} %get-tuple-element.10), kind=kLoop, calls=%fused_computation | loop fusion | flops 6291456 | bytes 16777216 | tf_op jit(solution)/shard_map/concatenate | solution.py:38
  17.0 0.0 all-reduce.4.cloned.1.call-update
  17.1 151.5 %all-reduce.6.cloned.1.call-done = (f32[256,1024]{1,0:T(8,128)}, f32[256,1024]{1,0:T(8,128)}, f32[256,1024]{1,0:T(8,128)}, f32[256,1024]{1,0:T(8,128)}) async-done(((f32[256,1024]{1,0:T(8,128)}, f32[256,1024]{1,0:T(8,128)}, f32[256,1024]{1,0:T(8,128)}, f32[256,1024]{1,0:T(8,128)}), (f32[256,1024]{1,0:T(8,128)}, f32[256,1024]{1,0:T(8,128)}, f32[256,1024]{1,0:T(8,128)}, ...) | async-done | bytes 4194320 | tf_op jit(solution)/shard_map/psum | solution.py:11
  168.6 129.3 %all-reduce.4.cloned.1.call-done = f32[2048,1024]{1,0:T(8,128)} async-done(((f32[2048,1024]{1,0:T(8,128)}), f32[2048,1024]{1,0:T(8,128)}) %all-reduce.4.cloned.1.call-update) | async-done | bytes 8388624 | tf_op jit(solution)/shard_map/psum | solution.py:38
  297.8 32.3 %multiply_reduce_fusion = (f32[]{:T(128)}, f32[2048,1024]{1,0:T(8,128)}) fusion(f32[2048,1024]{1,0:T(8,128)} %all-reduce.4.cloned.1.call-done, f32[256,1024]{1,0:T(8,128)} %get-tuple-element.2, f32[256,1024]{1,0:T(8,128)} %get-tuple-element.3, f32[256,1024]{1,0:T(8,128)} %get-tuple-element.4, f32[256,1024]{1,0:T(8,128)} %get-tuple-element.5), kind=kOutput, calls=%fused_computation.1 | convolution fusion | flops 25777143808 | bytes 20971524 | tf_op jit(solution)/shard_map/dot_general | solution.py:28
  330.2 39.6 %psum.47 = f32[]{:T(128)} all-reduce(f32[]{:T(128)} %get-tuple-element.14), channel_id=1, replica_groups=mesh['row'=4,'col'=8] {'row','col'}, use_global_device_ids=true, to_apply=%region_6.7 | all-reduce | flops 1 | bytes 8 | tf_op jit(solution)/shard_map/psum | solution.py:41
Async XLA Ops:
  7.2 161.4 %all-reduce.6.cloned.1.call-start = ((), (), s32[]{:S(2)}) async-start(), calls=%async_computation.1 | async-start | bytes 8388608 | tf_op jit(solution)/shard_map/psum | solution.py:11
  10.7 287.2 %all-reduce.4.cloned.1.call-start = ((), (), s32[]{:S(2)}) async-start(), calls=%async_computation | async-start | bytes 16777216 | tf_op jit(solution)/shard_map/psum | solution.py:38
Sparse Core Ops, SparseCore 0:
  10.8 157.7 all-reduce.5
  172.6 125.1 all-reduce.3
where the time goes:
time: 379 us; the launch traced here: 378 us
  waiting for transfers between devices  281 us (74%)
  blocking collectives  39.6 us (10%)
  matrix products  32.3 us (9%)
  between operations  15.9 us (4%)
  other arithmetic  9.73 us (3%)
    psum x1, waiting for transfers between devices, broadcast(): return lax.psum(kept, axis)  152 us
    psum x1, waiting for transfers between devices, body(): stacked = lax.psum(jnp.concatenate(slots, axis=1), 'col')  129 us
    psum x1, blocking collectives, body(): total = lax.psum(jnp.sum(squared * squared), ('row', 'col'))  39.6 us
    dot_general x1, matrix products, product(): jnp.dot(left, right, preferred_element_type=jnp.float32, precision=lax.Pr...  32.3 us
  transfers between devices with their start and end apart: 2, of which 2 were waited for; matrix products, arithmetic and copies ran while one was open for 2% of the time, Pallas kernels for 0%

commit v1 on v0

--- a/solution.py
+++ b/solution.py
@@ -8,7 +8,7 @@
 
 def broadcast(value, axis, source):
     kept = jnp.where(lax.axis_index(axis) == source, value, 0).astype(value.dtype)
-    return lax.psum(kept, axis)
+    return jnp.sum(lax.all_gather(kept, axis), axis=0)
 
 
 def offsets(matrix, step):

time: 379 us -> 421 us (1.11)
  waiting for transfers between devices: 281 us -> 311 us
  other arithmetic: 9.73 us -> 21.7 us
    all_gather x0 -> x4, waiting for transfers between devices: none -> 309 us  [broadcast(): return jnp.sum(lax.all_gather(kept, axis), axis=0)]
    psum x1 -> x0, waiting for transfers between devices: 152 us -> none  [broadcast(): return lax.psum(kept, axis)]
    psum x1, waiting for transfers between devices: 129 us -> 0.01 us  [body(): stacked = lax.psum(jnp.concatenate(slots, axis=1), 'col')]
    reduce_sum x0 -> x4, other arithmetic: none -> 11.9 us  [broadcast(): return jnp.sum(lax.all_gather(kept, axis), axis=0)]
  transfers between devices with their start and end apart: 2 -> 5, of which waited for: 2 -> 4; matrix products, arithmetic and copies ran while one was open for 2% -> 4% of each run, Pallas kernels for 0% -> 0%
where the time goes in v1:
time: 421 us
  waiting for transfers between devices  311 us (74%)
  blocking collectives  38.9 us (9%)
  matrix products  31.7 us (8%)
  other arithmetic  21.7 us (5%)
  between operations  17.1 us (4%)
    all_gather x4, waiting for transfers between devices, broadcast(): return jnp.sum(lax.all_gather(kept, axis), axis=0)  309 us
    psum x1, blocking collectives, body(): total = lax.psum(jnp.sum(squared * squared), ('row', 'col'))  38.9 us
    dot_general x1, matrix products, product(): jnp.dot(left, right, preferred_element_type=jnp.float32, precision=lax.Pr...  31.7 us
    reduce_sum x4, other arithmetic, broadcast(): return jnp.sum(lax.all_gather(kept, axis), axis=0)  11.9 us
  transfers between devices with their start and end apart: 5, of which 4 were waited for; matrix products, arithmetic and copies ran while one was open for 4% of the time, Pallas kernels for 0%

profile of v1, /device:TPU:0, one launch (start us, length us, event | category | flops | bytes accessed | tf_op | source)
XLA Modules:
  0.0 420.9 jit_solution(2547100847027480211)
XLA Ops:
  8.0 0.0 all-gather.9.cloned.1.call-start
  8.1 3.5 slice_select_fusion.7
  11.6 0.0 all-gather.9.cloned.1.call-update
  11.6 0.0 all-gather.11.cloned.1.call-start
  11.6 0.7 all-gather.11.cloned.1.call-update
  12.3 0.0 all-gather.13.cloned.1.call-start
  12.4 0.7 all-gather.13.cloned.1.call-update
  13.1 0.0 all-gather.15.cloned.1.call-start
  13.1 0.5 all-gather.15.cloned.1.call-update
  13.7 0.0 all-reduce.2.cloned.1.call-start
  13.7 2.2 slice_select_fusion.3
  16.0 4.1 pad_maximum_fusion
  20.0 0.0 all-reduce.2.cloned.1.call-update
  20.0 75.2 %all-gather.9.cloned.1.call-done = f32[1024,1024]{1,0:T(8,128)} async-done(((f32[256,1024]{1,0:T(8,128)}), f32[1024,1024]{1,0:T(8,128)}) %all-gather.9.cloned.1.call-update) | async-done | bytes 4194320 | tf_op jit(solution)/shard_map/all_gather | solution.py:11
  95.2 2.7 reduce_sum.45
  97.9 78.1 %all-gather.11.cloned.1.call-done = f32[1024,1024]{1,0:T(8,128)} async-done(((f32[256,1024]{1,0:T(8,128)}), f32[1024,1024]{1,0:T(8,128)}) %all-gather.11.cloned.1.call-update) | async-done | bytes 4194320 | tf_op jit(solution)/shard_map/all_gather | solution.py:11
  176.0 2.7 reduce_sum.46
  178.8 78.1 %all-gather.13.cloned.1.call-done = f32[1024,1024]{1,0:T(8,128)} async-done(((f32[256,1024]{1,0:T(8,128)}), f32[1024,1024]{1,0:T(8,128)}) %all-gather.13.cloned.1.call-update) | async-done | bytes 4194320 | tf_op jit(solution)/shard_map/all_gather | solution.py:11
  256.9 2.7 reduce_sum.47
  259.6 78.0 %all-gather.15.cloned.1.call-done = f32[1024,1024]{1,0:T(8,128)} async-done(((f32[256,1024]{1,0:T(8,128)}), f32[1024,1024]{1,0:T(8,128)}) %all-gather.15.cloned.1.call-update) | async-done | bytes 4194320 | tf_op jit(solution)/shard_map/all_gather | solution.py:11
  337.5 3.8 reduce_sum.48
  341.3 0.0 all-reduce.2.cloned.1.call-done
  341.3 31.7 %multiply_reduce_fusion = (f32[]{:T(128)}, f32[2048,1024]{1,0:T(8,128)}) fusion(f32[2048,1024]{1,0:T(8,128)} %all-reduce.2.cloned.1.call-done, f32[256,1024]{1,0:T(8,128)} %reduce_sum.48, f32[256,1024]{1,0:T(8,128)S(1)} %reduce_sum.47, f32[256,1024]{1,0:T(8,128)S(1)} %reduce_sum.46, f32[256,1024]{1,0:T(8,128)S(1)} %reduce_sum.45), kind=kOutput, calls=%fused_computation.1 | convolution fusion | flops 25777143808 | bytes 20971524 | tf_op jit(solution)/shard_map/dot_general | solution.py:28
  373.0 38.9 %psum.15 = f32[]{:T(128)} all-reduce(f32[]{:T(128)} %get-tuple-element.10), channel_id=1, replica_groups=mesh['row'=4,'col'=8] {'row','col'}, use_global_device_ids=true, to_apply=%region_6.7 | all-reduce | flops 1 | bytes 8 | tf_op jit(solution)/shard_map/psum | solution.py:41
Async XLA Ops:
  8.0 87.2 %all-gather.9.cloned.1.call-start = ((), (), s32[]{:S(2)}) async-start(), calls=%async_computation.1 | async-start | bytes 5242880 | tf_op jit(solution)/shard_map/all_gather | solution.py:11
  11.6 164.4 %all-gather.11.cloned.1.call-start = ((), (), s32[]{:S(2)}) async-start(), calls=%async_computation.2 | async-start | bytes 5242880 | tf_op jit(solution)/shard_map/all_gather | solution.py:11
  12.3 244.5 %all-gather.13.cloned.1.call-start = ((), (), s32[]{:S(2)}) async-start(), calls=%async_computation.3 | async-start | bytes 5242880 | tf_op jit(solution)/shard_map/all_gather | solution.py:11
  13.1 324.5 %all-gather.15.cloned.1.call-start = ((), (), s32[]{:S(2)}) async-start(), calls=%async_computation.4 | async-start | bytes 5242880 | tf_op jit(solution)/shard_map/all_gather | solution.py:11
  13.7 327.7 %all-reduce.2.cloned.1.call-start = ((), (), s32[]{:S(2)}) async-start(), calls=%async_computation | async-start | bytes 16777216 | tf_op jit(solution)/shard_map/psum | solution.py:38
Sparse Core Ops, SparseCore 0:
  11.7 83.4 all-gather.8
  96.8 79.2 all-gather.10
  177.6 79.2 all-gather.12
  258.3 79.2 all-gather.14
Sparse Core Ops, SparseCore 1:
  20.1 128.6 all-reduce.1
